TPU v7x, 256 devices: a whole 4x4x8 slice. The times are simulated.
256 devices in a mesh: grp: 8 (over y_lo, x), mem: 32 (over z, y_hi, core).
Axes of the slice: x: 4, y: 4 (y_hi: 2, y_lo: 2; y = y_hi * 2 + y_lo), z: 8, core: 2. Of those that a mesh axis runs over, the one named last changes fastest.
Arguments:
- factors: bfloat16 [256, 512, 2048], P(('grp', 'mem')), may hold values from -1 to 1
- occ_energy: bfloat16 [256], P(('grp', 'mem')), may hold values from -1.5 to -0.29882812
- vir_energy: bfloat16 [512], replicated, may hold values from 0.3984375 to 3
- pair_code: int32 [8, 32, 3], P('grp'), may hold values from 0 to 2
- pair_count: int32 [8, 32], P('grp'), may hold values from 1 to 3
Outputs:
- aux_density: bfloat16 [256, 512, 2048], P(('grp', 'mem'))
- lagrangian: bfloat16 [256, 512, 2048], P(('grp', 'mem'))
Inputs may be any that keep to these rules, and one draw needn't show every extreme that they name: `pair_code`: only the first pair_count entries of a device's list are read; entries may repeat.
All inputs are finite; a program needn't handle non-finite values.
Results may differ from a plain program's by a relative error of at most 0.0056.
Values may be sent and summed in bfloat16 or wider, within the bound.
A program may use at most 128 MiB of HBM per device.

v0:
```python
import jax
import jax.numpy as jnp
from jax import lax
from jax.sharding import PartitionSpec as P

OCC_DEV = 1
ROUNDS = 2


def partner(value, axis, distance):
    mask = 2**distance
    pairs = [(source, source ^ mask) for source in range(lax.axis_size(axis))]
    return lax.ppermute(value, axis, pairs)


def padded_to(lines, length):
    spare = -len(lines) % length
    return jnp.pad(lines, [(0, spare)] + [(0, 0)] * (lines.ndim - 1))


def from_everyone(value, axis):
    copies = jnp.broadcast_to(value, (lax.axis_size(axis), *value.shape))
    return lax.all_to_all(copies, axis, split_axis=0, concat_axis=0, tiled=True)


def joined_along(blocks, dim):
    lengths = list(blocks.shape[1:])
    lengths[dim] *= blocks.shape[0]
    return jnp.moveaxis(blocks, 0, dim).reshape(lengths)


def collect(value, axis, dim):
    blocks = from_everyone(value, axis)
    return joined_along(blocks, dim)


def cut_along(value, dim, length):
    before, after = (value.shape[:dim], value.shape[dim + 1 :])
    return jnp.moveaxis(value.reshape(*before, length, -1, *after), dim, 0)


def sum_at_owner(value, axis, dim):
    length = lax.axis_size(axis)
    blocks = lax.all_to_all(cut_along(value, dim, length), axis, 0, 0, tiled=True)
    return jnp.sum(blocks.astype(jnp.float32), axis=0)


def total_of(value, axes):
    lines = value.reshape(-1, value.shape[-1])
    padded = padded_to(lines, lax.axis_size(axes))
    whole = collect(sum_at_owner(padded, axes, 0).astype(jnp.bfloat16), axes, 0)
    return lax.slice_in_dim(whole, 0, len(lines)).reshape(value.shape).astype(jnp.float32)


def decode_pair(code):
    round_no = code // (OCC_DEV * OCC_DEV)
    left_orb = code // OCC_DEV % OCC_DEV
    right_orb = code % OCC_DEV
    return (round_no, left_orb, right_orb)


def add_at(target, indices, contribution):
    zero_index = jnp.zeros((), jnp.int32)
    anchor = tuple(indices) + (zero_index,) * contribution.ndim
    extent = (1,) * len(indices) + contribution.shape
    current = lax.dynamic_slice(target, anchor, extent)
    return lax.dynamic_update_slice(target, current + contribution.reshape(extent), anchor)


def outer_terms(amp_tile):
    return lax.dot_general(
        amp_tile, amp_tile, (((1,), (1,)), ((), ())), preferred_element_type=jnp.float32
    )


def near_product(amp_tile, right_block):
    return jnp.dot(amp_tile, right_block, preferred_element_type=jnp.float32)


def far_product(amp_tile, left_block):
    return lax.dot_general(
        amp_tile, left_block, (((0,), (0,)), ((), ())), preferred_element_type=jnp.float32
    )


def per_device(factors, occ_energy, vir_energy, pair_code, pair_count):
    virtual = vir_energy.astype(jnp.float32)
    my_place = lax.axis_index("mem")
    group_codes = pair_code[0]
    group_counts = pair_count[0]
    my_codes = lax.dynamic_index_in_dim(group_codes, my_place, 0, keepdims=False)
    live_count = lax.dynamic_index_in_dim(group_counts, my_place, 0, keepdims=False)
    blocks_all = [factors]
    energy_list = [occ_energy]
    for round_idx in range(ROUNDS):
        visitor, visitor_energy = partner((factors, occ_energy), "mem", round_idx)
        blocks_all.append(visitor)
        energy_list.append(visitor_energy)
    stacked = jnp.stack(blocks_all)
    energy_all = jnp.stack(energy_list).astype(jnp.float32)
    vir_count = factors.shape[1]
    density_zero = jnp.zeros((vir_count, vir_count), jnp.float32)

    def pair_terms(slot_no):
        round_no, left_orb, right_orb = decode_pair(my_codes[slot_no])
        left_block = stacked[0, left_orb]
        right_block = stacked[round_no, right_orb]
        integrals = lax.dot_general(
            left_block, right_block, (((1,), (1,)), ((), ())), preferred_element_type=jnp.float32
        )
        denominator = (
            virtual[:, None]
            + virtual[None, :]
            - energy_all[0, left_orb]
            - energy_all[round_no, right_orb]
        )
        amp_tile = (integrals / denominator).astype(jnp.bfloat16)
        return (round_no, left_orb, right_orb, left_block, right_block, amp_tile)

    def pair_step(slot_no, carry_pair):
        density, totals = carry_pair
        round_no, left_orb, right_orb, left_block, right_block, amp_tile = pair_terms(slot_no)
        density = density + outer_terms(amp_tile)
        totals = add_at(
            totals, (jnp.zeros((), jnp.int32), left_orb), near_product(amp_tile, right_block)
        )
        totals = add_at(totals, (round_no, right_orb), far_product(amp_tile, left_block))
        return (density, totals)

    totals_zero = jnp.zeros((ROUNDS + 1,) + factors.shape, jnp.float32)
    density, totals = lax.fori_loop(0, live_count, pair_step, (density_zero, totals_zero))
    gathered = totals[0]
    for round_idx in range(ROUNDS):
        gathered = gathered + partner(
            totals[round_idx + 1].astype(jnp.bfloat16), "mem", round_idx
        ).astype(jnp.float32)
    density = total_of(density.astype(jnp.bfloat16), "mem")
    density = lax.psum(density, "grp")
    density_scale = 1.0 / (8.0 * lax.axis_size("grp") * lax.axis_size("mem"))
    density_tile = (density * density_scale).astype(jnp.bfloat16)
    lagrangian = jnp.einsum(
        "ab,kbp->kap", density_tile, factors, preferred_element_type=jnp.float32
    )
    return (gathered.astype(jnp.bfloat16), lagrangian.astype(jnp.bfloat16))


def solution(mesh):
    in_specs = (
        P(("grp", "mem"), None, None),
        P(("grp", "mem")),
        P(),
        P("grp", None, None),
        P("grp", None),
    )
    out_specs = (P(("grp", "mem"), None, None), P(("grp", "mem"), None, None))
    return jax.shard_map(
        per_device, mesh=mesh, in_specs=in_specs, out_specs=out_specs, check_vma=False
    )
```

profile of v0, /device:TPU:16, one launch (start us, length us, event | category | flops | bytes accessed | tf_op | source)
XLA Modules:
  0.0 300.3 jit_solution(17205998147566589617)
XLA Ops:
  7.2 0.0 copy-start
  7.2 0.1 collective-permute-start
  7.3 2.1 collective-permute-start.1
  9.4 1.5 collective-permute-start.3
  10.9 0.0 collective-permute-start.2
  11.6 0.7 convert_element_type.79
  12.3 1.2 constant_dynamic-slice_fusion.1
  13.5 0.0 copy-done
  13.5 0.2 dynamic-slice_reduce_fusion
  13.7 43.4 %collective-permute-done.3 = bf16[1]{0:T(256)(128)(2,1)} collective-permute-done((bf16[1]{0:T(256)(128)(2,1)}, bf16[1]{0:T(256)(128)(2,1)}, u32[]{:S(2)}, u32[]{:S(2)}) %collective-permute-start.3) | collective-permute-done | bytes 34 | tf_op jit(solution)/shard_map/ppermute | solution.py:13
  57.1 0.0 collective-permute-done.2
  57.1 1.4 maximum_convert_fusion
  58.5 0.0 collective-permute-done
  58.5 0.0 collective-permute-done.1
  58.5 5.5 %pad_maximum_fusion = bf16[3,1,512,2048]{3,2,1,0:T(8,128)(2,1)} fusion(bf16[1,1,512,2048]{3,2,1,0:T(8,128)(2,1)} %bitcast.11, bf16[1,1,512,2048]{3,2,1,0:T(8,128)(2,1)S(1)} %bitcast.97, bf16[1,1,512,2048]{3,2,1,0:T(8,128)(2,1)} %bitcast.96), kind=kLoop, calls=%fused_computation.19 | loop fusion | flops 6291456 | bytes 12582912 | tf_op jit(solution)/shard_map/stack | solution.py:99
  64.0 0.1 broadcast_in_dim.11
  64.1 6.1 %broadcast_in_dim.12 = f32[3,1,512,2048]{3,2,1,0:T(8,128)} broadcast(f32[]{:T(128)} %constant.76.clone.1), dimensions={} | broadcast | bytes 12582916 | tf_op jit(solution)/shard_map/broadcast_in_dim | solution.py:130
  70.2 20.0 %while.14 = (s32[]{:T(128)}, f32[512,512]{1,0:T(8,128)S(1)}, f32[3,1,512,2048]{3,2,1,0:T(8,128)}, s32[]{:T(128)}, s32[3]{0:T(128)S(1)}, /*index=5*/bf16[3,1,512,...) while((s32[]{:T(128)}, f32[512,512]{1,0:T(8,128)S(1)}, ...), condition=%wide.region_1.2_spmd, body=%wide.region_0.1_spmd.sunk | while | flops 3493330944 | bytes 155194704 | solution.py:131
  70.9 0.7 dynamic_slice.94
  73.6 0.6 fusion.52
  74.2 0.0 copy-start.1
  74.2 0.0 copy-start.3
  74.2 6.0 %divide_convert_fusion.2 = bf16[512,512]{0,1:T(8,128)(2,1)S(1)} fusion(bf16[3,1,512,2048]{3,2,1,0:T(8,128)(2,1)} %get-tuple-element.212, s32[]{:T(128)S(6)} %select_n.46, f32[]{:T(128)} %bitcast.93, f32[]{:T(128)} %bitcast.94, f32[512]{0:T(512)S(1)} %get-tuple-element.213), kind=kOutput, calls=%fused_computation.15.clone.1 | convolution fusion | flops 1075052544 | bytes 4723716 | tf_op jit(solution)/shard_map/while/body/dot_general | solution.py:108
  80.2 0.5 convolution_add_fusion.2
  80.7 0.0 copy-done.1
  80.7 1.1 copy-done.3
  81.8 1.6 fusion.53
  83.4 1.6 fusion.54
  85.0 0.0 copy-start.2
  85.0 4.5 %copy-done.2 = f32[3,1,512,2048]{3,2,1,0:T(8,128)} copy-done((f32[3,1,512,2048]{3,2,1,0:T(8,128)}, f32[3,1,512,2048]{3,2,1,0:T(8,128)S(1)}, u32[]{:S(2)}) %copy-start.2) | copy-done | bytes 12582936 | tf_op jit(solution)/shard_map/while
  90.2 0.9 convert_element_type.86
  91.1 50.3 %all-to-all-start = ((bf16[32,16,512]{2,1,0:T(8,128)(2,1)}), bf16[32,16,512]{2,1,0:T(8,128)(2,1)}, u32[]{:S(2)}, u32[]{:S(2)}) async-start(bf16[32,16,512]{2,1,0:T(8,128)(2,1)} %bitcast.18), calls=%async_computation | async-start | bytes 1048576 | tf_op jit(solution)/shard_map/all_to_all | solution.py:44
  141.4 0.0 all-reduce.2.cloned.1.call-start
  141.4 5.6 %convert.6 = bf16[3,1,512,2048]{3,2,1,0:T(8,128)(2,1)S(1)} convert(f32[3,1,512,2048]{3,2,1,0:T(8,128)} %get-tuple-element.109) | non-fusion elementwise | flops 3145728 | bytes 18874368 | tf_op jit(solution)/shard_map/convert.3
  147.0 2.3 slice_bitcast_fusion.1
  149.3 0.1 collective-permute-start.4
  149.4 0.4 collective-permute-start.5
  149.8 9.3 %all-to-all-done = bf16[32,16,512]{2,1,0:T(8,128)(2,1)} async-done(((bf16[32,16,512]{2,1,0:T(8,128)(2,1)}), bf16[32,16,512]{2,1,0:T(8,128)(2,1)}, u32[]{:S(2)}, u32[]{:S(2)}) %all-to-all-start) | async-done | bytes 524320 | tf_op jit(solution)/shard_map/all_to_all | solution.py:44
  159.1 1.1 reduce_sum.12
  160.2 0.1 broadcast_in_dim.13
  160.3 44.8 %all_to_all.10 = bf16[32,16,512]{2,1,0:T(8,128)(2,1)S(1)} all-to-all(bf16[32,16,512]{2,1,0:T(8,128)(2,1)S(1)} %broadcast_in_dim.13), channel_id=1, replica_groups=mesh['grp'=8,'mem'=32] {'mem'}, dimensions={0} | all-to-all | bytes 1048576 | tf_op jit(solution)/shard_map/all_to_all | solution.py:23
  205.1 1.1 bitcast_convert_fusion
  206.2 0.0 all-reduce.2.cloned.1.call-update
  206.2 0.0 collective-permute-done.4
  206.2 0.0 collective-permute-done.5
  206.2 5.2 %fusion.23 = bf16[1,512,2048]{2,1,0:T(8,128)(2,1)} fusion(bf16[1,512,2048]{2,1,0:T(8,128)(2,1)} %collective-permute-done.5, bf16[1,512,2048]{2,1,0:T(8,128)(2,1)S(1)} %collective-permute-done.4, f32[3,1,512,2048]{3,2,1,0:T(8,128)} %get-tuple-element.109), kind=kLoop, calls=%fused_computation.22 | loop fusion | flops 5242880 | bytes 10485760 | tf_op jit(solution)/shard_map/convert_element_type | solution.py:144
  211.5 77.5 %all-reduce.2.cloned.1.call-done = f32[512,512]{1,0:T(8,128)} async-done(((f32[512,512]{1,0:T(8,128)}), f32[512,512]{1,0:T(8,128)}) %all-reduce.2.cloned.1.call-update) | async-done | bytes 1048592 | tf_op jit(solution)/shard_map/psum | solution.py:138
  288.9 4.5 %fusion.24 = bf16[1,512,2048]{2,1,0:T(8,128)(2,1)} fusion(bf16[1,512,2048]{2,1,0:T(8,128)(2,1)} %param.7, f32[512,512]{1,0:T(8,128)} %all-reduce.2.cloned.1.call-done), kind=kOutput, calls=%fused_computation.24 | convolution fusion | flops 1075314688 | bytes 5242880 | tf_op jit(solution)/shard_map/ab,kbp->kap/dot_general | solution.py:141
Async XLA Ops:
  7.2 6.3 %copy-start = (s32[1,32,3]{1,0,2:T(1,128)S(1)}, s32[1,32,3]{1,0,2:T(1,128)}, u32[]{:S(2)}) copy-start(s32[1,32,3]{1,0,2:T(1,128)} %param.10) | copy-start | bytes 1156
  7.2 51.3 %collective-permute-start = (bf16[1,512,2048]{2,1,0:T(8,128)(2,1)}, bf16[1,512,2048]{2,1,0:T(8,128)(2,1)S(1)}, u32[]{:S(2)}, u32[]{:S(2)}) collective-permute-start(bf16[1,512,2048]{2,1,0:T(8,128)(2,1)} %param.7), channel_id=1, source_target_pairs={{0,1},{1,0},{2,3},{3,2},{4,5},{5,4},{6,7},{7,6},{8,9},{9,8},{10,11... | collective-permute-start | bytes 6291464 | tf_op jit(solution)/shard_map/ppermute | solution.py:13
  7.3 51.2 %collective-permute-start.1 = (bf16[1,512,2048]{2,1,0:T(8,128)(2,1)}, bf16[1,512,2048]{2,1,0:T(8,128)(2,1)}, u32[]{:S(2)}, u32[]{:S(2)}) collective-permute-start(bf16[1,512,2048]{2,1,0:T(8,128)(2,1)} %param.7), channel_id=1, source_target_pairs={{0,2},{1,3},{2,0},{3,1},{4,6},{5,7},{6,4},{7,5},{8,10},{9,11},{10,... | collective-permute-start | bytes 6291464 | tf_op jit(solution)/shard_map/ppermute | solution.py:13
  9.4 47.7 %collective-permute-start.3 = (bf16[1]{0:T(256)(128)(2,1)}, bf16[1]{0:T(256)(128)(2,1)}, u32[]{:S(2)}, u32[]{:S(2)}) collective-permute-start(bf16[1]{0:T(256)(128)(2,1)} %param.8), channel_id=1, source_target_pairs={{0,2},{1,3},{2,0},{3,1},{4,6},{5,7},{6,4},{7,5},{8,10},{9,11},{10,... | collective-permute-start | bytes 14 | tf_op jit(solution)/shard_map/ppermute | solution.py:13
  10.9 46.2 %collective-permute-start.2 = (bf16[1]{0:T(256)(128)(2,1)}, bf16[1]{0:T(256)(128)(2,1)}, u32[]{:S(2)}, u32[]{:S(2)}) collective-permute-start(bf16[1]{0:T(256)(128)(2,1)} %param.8), channel_id=1, source_target_pairs={{0,1},{1,0},{2,3},{3,2},{4,5},{5,4},{6,7},{7,6},{8,9},{9,8},{10,11... | collective-permute-start | bytes 14 | tf_op jit(solution)/shard_map/ppermute | solution.py:13
  74.2 6.5 %copy-start.1 = (f32[3,1,512,2048]{3,2,1,0:T(8,128)S(1)}, f32[3,1,512,2048]{3,2,1,0:T(8,128)}, u32[]{:S(2)}) copy-start(f32[3,1,512,2048]{3,2,1,0:T(8,128)} %get-tuple-element.198) | copy-start | bytes 37748740 | tf_op jit(solution)/shard_map/while
  74.2 7.6 %copy-start.3 = (bf16[3,1,512,2048]{3,2,1,0:T(8,128)(2,1)S(1)}, bf16[3,1,512,2048]{3,2,1,0:T(8,128)(2,1)}, u32[]{:S(2)}) copy-start(bf16[3,1,512,2048]{3,2,1,0:T(8,128)(2,1)} %get-tuple-element.212) | copy-start | bytes 18874372 | tf_op jit(solution)/shard_map/while
  85.0 4.5 %copy-start.2 = (f32[3,1,512,2048]{3,2,1,0:T(8,128)}, f32[3,1,512,2048]{3,2,1,0:T(8,128)S(1)}, u32[]{:S(2)}) copy-start(f32[3,1,512,2048]{3,2,1,0:T(8,128)S(1)} %fusion.54) | copy-start | bytes 37748740 | tf_op jit(solution)/shard_map/while
  91.1 68.0 %all-to-all-start = ((bf16[32,16,512]{2,1,0:T(8,128)(2,1)}), bf16[32,16,512]{2,1,0:T(8,128)(2,1)}, u32[]{:S(2)}, u32[]{:S(2)}) async-start(bf16[32,16,512]{2,1,0:T(8,128)(2,1)} %bitcast.18), calls=%async_computation | async-start | bytes 1048576 | tf_op jit(solution)/shard_map/all_to_all | solution.py:44
  141.4 147.5 %all-reduce.2.cloned.1.call-start = ((), (), s32[]{:S(2)}) async-start(), calls=%async_computation.2 | async-start | bytes 2097152 | tf_op jit(solution)/shard_map/psum | solution.py:138
  149.3 56.9 %collective-permute-start.4 = (bf16[1,512,2048]{2,1,0:T(8,128)(2,1)}, bf16[1,512,2048]{2,1,0:T(8,128)(2,1)S(1)}, u32[]{:S(2)}, u32[]{:S(2)}) collective-permute-start(bf16[1,512,2048]{2,1,0:T(8,128)(2,1)} %get-tuple-element.129), channel_id=1, source_target_pairs={{0,1},{1,0},{2,3},{3,2},{4,5},{5,4},{6,7},{7,6},{8,9},{9,8},{10,11... | collective-permute-start | bytes 6291464 | tf_op jit(solution)/shard_map/ppermute | solution.py:13
  149.4 56.8 %collective-permute-start.5 = (bf16[1,512,2048]{2,1,0:T(8,128)(2,1)}, bf16[1,512,2048]{2,1,0:T(8,128)(2,1)}, u32[]{:S(2)}, u32[]{:S(2)}) collective-permute-start(bf16[1,512,2048]{2,1,0:T(8,128)(2,1)} %get-tuple-element.130), channel_id=1, source_target_pairs={{0,2},{1,3},{2,0},{3,1},{4,6},{5,7},{6,4},{7,5},{8,10},{9,11},{10,... | collective-permute-start | bytes 6291464 | tf_op jit(solution)/shard_map/ppermute | solution.py:13
Sparse Core Ops, SparseCore 0:
  206.3 82.5 all-reduce.1
where the time goes:
time: 301 us; the launch traced here: 300 us
  waiting for transfers between devices  130 us (43%)
  starting transfers between devices  54.6 us (18%)
  blocking collectives  44.8 us (15%)
  other arithmetic  21.4 us (7%)
  local copies, waits for them, and re-layouts  17 us (6%)
  between operations  14.8 us (5%)
  matrix products  14.2 us (5%)
  loops' own time  3.39 us (1%)
    psum x1, waiting for transfers between devices, per_device(): density = lax.psum(density, 'grp')  77.5 us
    all_to_all x1, starting transfers between devices, sum_at_owner(): lax.all_to_all(cut_along(value, dim, length), axis, 0, 0, tiled=True)  50.3 us
    all_to_all x1, blocking collectives, from_everyone(): return lax.all_to_all(copies, axis, split_axis=0, concat_axis=0, tiled=True)  44.8 us
    ppermute x6, waiting for transfers between devices, partner(): return lax.ppermute(value, axis, pairs)  43.4 us
    all_to_all x1, waiting for transfers between devices, sum_at_owner(): lax.all_to_all(cut_along(value, dim, length), axis, 0, 0, tiled=True)  9.28 us
    broadcast_in_dim x1, local copies, waits for them, and re-layouts, per_device(): totals_zero = jnp.zeros((ROUNDS + 1,) + factors.shape, jnp.float32)  6.12 us
  transfers between devices with their start and end apart: 8, of which 3 were waited for; matrix products, arithmetic and copies ran while one was open for 6% of the time, Pallas kernels for 0%

commit v1 on v0

v1 whole, which is shorter than its diff:
```python
import functools

import jax
import jax.numpy as jnp
from jax import lax
from jax.experimental import pallas as pl
from jax.experimental.pallas import tpu as pltpu
from jax.sharding import PartitionSpec as P

MESH = pl.DeviceIdType.MESH
NX, NY, NZ = 4, 4, 8
CHUNKS = 16
FIRST = 7
LEAD = 2
F32, BF16 = jnp.float32, jnp.bfloat16


def nt(a, b):
    return lax.dot_general(a, b, (((1,), (1,)), ((), ())), preferred_element_type=F32)


def tn(a, b):
    return lax.dot_general(a, b, (((0,), (0,)), ((), ())), preferred_element_type=F32)


def nn(a, b):
    return jnp.dot(a, b, preferred_element_type=F32)


def body(
    b_own, table, code, count,
    gamma_out, lag_out,
    ball, tall, ens, vsum, acc, dens, dl_send, dl_recv, xs, xr, zs, zr, ys, yr, dfull,
    pair_s, pair_r, bulk_s, bulk_r, en_s, en_r, dl_s, dl_rs,
    x_s, x_r, z_s, z_r, y_s, y_r, za_s, za_r, xa_s, xa_r, fw_s, fw_r,
):
    V, A = b_own.shape
    g, m = lax.axis_index("grp"), lax.axis_index("mem")
    x, ylo = lax.rem(g, NX), g // NX
    core, yhi, z = lax.rem(m, 2), lax.rem(m // 2, 2), m // 4
    y = yhi * 2 + ylo
    mate = m + 1 - 2 * core
    far = m + 2 - 4 * yhi
    early = core == yhi
    late = core != yhi
    rows_x, rows_z = V // NX, V // NX // NZ

    def to_x(d):
        return {"grp": ylo * NX + lax.rem(x + d, NX), "mem": m}

    def to_z(d):
        return {"grp": g, "mem": lax.rem(z + d, NZ) * 4 + yhi * 2 + core}

    def to_y(d):
        other = lax.rem(y + d, NY)
        hi, lo = other // 2, lax.rem(other, 2)
        return {"grp": lo * NX + x, "mem": z * 4 + hi * 3}

    to_mate = {"grp": g, "mem": mate}
    to_far = {"grp": g, "mem": far}

    barrier = pltpu.get_barrier_semaphore()

    def greet(where):
        pl.semaphore_signal(barrier, inc=1, device_id=where, device_id_type=MESH)

    def remote(src, dst, send, recv, where):
        return pltpu.make_async_remote_copy(
            src_ref=src, dst_ref=dst, send_sem=send, recv_sem=recv, device_id=where, device_id_type=MESH
        )

    greet(to_mate)
    greet(to_far)

    @pl.when(early)
    def _():
        for d in range(1, NX):
            greet(to_x(d))
        for d in range(1, NZ):
            greet(to_z(d))
        for d in range(1, NY):
            greet(to_y(d))

    crows = V // CHUNKS

    def bulk(i):
        r = pl.ds(pl.multiple_of(i * crows, crows), crows)
        return remote(b_own.at[r], ball.at[1, r], bulk_s.at[i], bulk_r.at[i], to_far)

    def bulk_start(lo, hi):
        @pl.loop(lo, hi)
        def _(i):
            bulk(i).start()

    def bulk_wait(lo, hi):
        @pl.loop(lo, hi)
        def _(i):
            bulk(i).wait_recv()

    pair = remote(b_own, ball.at[0], pair_s, pair_r, to_mate)
    en1 = remote(table.at[8:16], ens.at[0], en_s.at[0], en_r.at[0], to_mate)
    en2 = remote(table.at[8:16], ens.at[1], en_s.at[1], en_r.at[1], to_far)

    @pl.when(late)
    def _():
        pl.semaphore_wait(barrier, 2)

    @pl.when(early)
    def _():
        pl.semaphore_wait(barrier, 2 + NX - 1 + NZ - 1 + NY - 1)

    en1.start()
    en2.start()

    @pl.when(late)
    def _():
        bulk_start(0, CHUNKS)

    pair.start()

    def lives(who, rnd):
        total = jnp.int32(0)
        for s in range(code.shape[2]):
            hit = jnp.logical_and(code[0, who, s] == rnd, s < count[0, who])
            total = total + jnp.where(hit, 1, 0)
        return total.astype(F32)

    c0, c1, c2 = lives(m, 0), lives(m, 1), lives(m, 2)
    d1, d2 = lives(mate, 1), lives(far, 2)

    for i in range(V // 128):
        column = jnp.broadcast_to(table[0:1, i * 128 : (i + 1) * 128], (128, 128)).T
        for j in range(V // 128):
            vsum[i * 128 : (i + 1) * 128, j * 128 : (j + 1) * 128] = column + table[0:1, j * 128 : (j + 1) * 128]

    acc[...] = jnp.zeros_like(acc)
    dens[...] = jnp.zeros_like(dens)
    own = table[8:9, 0:1]
    blocks = (b_own, ball.at[0], ball.at[1])

    def tile(r, lo, width, other):
        cols = pl.ds(pl.multiple_of(lo, 128), width)
        k = nt(b_own[...], blocks[r][cols, :])
        denominator = vsum[:, cols] - own - other
        tall[r, :, cols] = (k / denominator).astype(BF16)

    def gamma(r, lo, width, weight):
        rows = pl.ds(pl.multiple_of(lo, 128), width)

        @pl.loop(0, A // 256)
        def _(p):
            c = pl.ds(pl.multiple_of(p * 256, 256), 256)
            acc[:, c] = acc[:, c] + weight * nn(tall[r, :, rows], blocks[r][rows, c])

    def outer(r, lo, width, weight):
        cols = pl.ds(pl.multiple_of(lo, 128), width)

        @pl.loop(0, V // 256)
        def _(p):
            c = pl.ds(pl.multiple_of(p * 256, 256), 256)
            dens[:, c] = dens[:, c] + weight * nt(tall[r, :, cols], tall[r, c, cols])

    def inner(r, weight):
        @pl.loop(0, V // 256)
        def _(p):
            c = pl.ds(pl.multiple_of(p * 256, 256), 256)
            dens[:, c] = dens[:, c] + weight * tn(tall[r], tall[r, :, c])

    def whole(r, other, outer_weight, gamma_weight):
        @pl.loop(0, V // 256)
        def _(p):
            tile(r, p * 256, 256, other)

        outer(r, 0, V, outer_weight)
        gamma(r, 0, V, gamma_weight)

    whole(0, own, c0, c0 + c0)
    en1.wait_recv()
    pair.wait_recv()
    whole(1, ens[0, 0:1, 0:1], c1, c1 + d1)

    dl = remote(dl_send, dl_recv, dl_s, dl_rs, to_mate)

    @pl.when(late)
    def _():
        dl_send[...] = dens[...].astype(BF16)
        dl.start()

    en2.wait_recv()
    w2 = c2 + d2
    far_energy = ens[1, 0:1, 0:1]

    bulk_wait(0, CHUNKS // 2)
    tile(2, 0, 256, far_energy)

    @pl.when(early)
    def _():
        outer(2, 0, 256, c2)

    gamma(2, 0, 256, w2)
    bulk_wait(CHUNKS // 2, 3 * CHUNKS // 4)
    tile(2, 256, 128, far_energy)

    @pl.when(early)
    def _():
        outer(2, 256, 128, c2)

    gamma(2, 256, 128, w2)
    bulk_wait(3 * CHUNKS // 4, CHUNKS - LEAD)

    @pl.when(early)
    def _():
        bulk_start(0, FIRST)

    bulk_wait(CHUNKS - LEAD, CHUNKS)
    tile(2, 384, 128, far_energy)

    def block_x(d):
        return pl.ds(pl.multiple_of(lax.rem(x + d, NX) * rows_x, rows_x), rows_x)

    def block_z(d):
        return pl.ds(pl.multiple_of(lax.rem(z + d, NZ) * rows_z, rows_z), rows_z)

    def piece(d):
        return pl.ds(pl.multiple_of(x * rows_x + lax.rem(z + d, NZ) * rows_z, rows_z), rows_z)

    x_order = (1, 3, 2)
    z_order = (4, 3, 5, 2, 6, 1, 7)

    @pl.when(early)
    def _():
        outer(2, 384, 128, c2)
        inner(2, d2)
        dl.wait_recv()
        dens[...] = dens[...] + dl_recv[...].astype(F32)
        xs[...] = dens[...].astype(BF16)
        for d in x_order:
            remote(xs.at[block_x(d)], xr.at[d - 1], x_s.at[d - 1], x_r.at[d - 1], to_x(d)).start()

    gamma(2, 384, 128, w2)
    gamma_out[...] = acc[...].astype(BF16)

    def x_copy(d):
        return remote(xs.at[block_x(d)], xr.at[d - 1], x_s.at[d - 1], x_r.at[d - 1], to_x(d))

    def z_copy(d):
        return remote(zs.at[block_z(d)], zr.at[d - 1], z_s.at[d - 1], z_r.at[d - 1], to_z(d))

    def y_copy(d):
        return remote(ys, yr.at[d - 1], y_s.at[d - 1], y_r.at[d - 1], to_y(d))

    def za_copy(d):
        return remote(dfull.at[piece(0)], dfull.at[piece(0)], za_s.at[d - 1], za_r.at[d - 1], to_z(d))

    def za_arrival(d):
        r = piece(NZ - d)
        return remote(dfull.at[r], dfull.at[r], za_s.at[d - 1], za_r.at[d - 1], to_z(d))

    def xa_copy(d):
        r = block_x(0)
        return remote(dfull.at[r], dfull.at[r], xa_s.at[d - 1], xa_r.at[d - 1], to_x(d))

    def xa_arrival(d):
        r = block_x(NX - d)
        return remote(dfull.at[r], dfull.at[r], xa_s.at[d - 1], xa_r.at[d - 1], to_x(d))

    def fw_copy(d):
        r = block_x(lax.rem(NX - d, NX))
        return remote(dfull.at[r], dfull.at[r], fw_s.at[d], fw_r.at[d], to_mate)

    def lag(d):
        r = block_x(lax.rem(NX - d, NX))

        @pl.loop(0, A // 512)
        def _(p):
            c = pl.ds(pl.multiple_of(p * 512, 512), 512)
            lag_out[r, c] = nn(dfull[r, :], b_own[:, c]).astype(BF16)

    @pl.when(early)
    def _():
        for d in x_order:
            x_copy(d).wait_recv()
        sum_x = dens[block_x(0), :]
        for d in range(NX - 1):
            sum_x = sum_x + xr[d].astype(F32)
        dens[0:rows_x, :] = sum_x
        zs[...] = sum_x.astype(BF16)
        for d in z_order:
            z_copy(d).start()
        for d in z_order:
            z_copy(d).wait_recv()
        sum_z = dens[block_z(0), :]
        for d in range(NZ - 1):
            sum_z = sum_z + zr[d].astype(F32)
        ys[...] = sum_z.astype(BF16)
        for d in (2, 1, 3):
            y_copy(d).start()
        bulk_start(FIRST, CHUNKS)
        for d in (2, 1, 3):
            y_copy(d).wait_recv()
        total = sum_z
        for d in range(NY - 1):
            total = total + yr[d].astype(F32)
        dfull[piece(0), :] = (total * (1.0 / (8.0 * 2 * NX * NY * NZ))).astype(BF16)
        for d in z_order:
            za_copy(d).start()
        for d in z_order:
            za_arrival(d).wait_recv()
        for d in x_order:
            xa_copy(d).start()
        fw_copy(0).start()
        lag(0)
        for d in x_order:
            xa_arrival(d).wait_recv()
            fw_copy(d).start()
            lag(d)

    @pl.when(late)
    def _():
        for d in (0,) + x_order:
            fw_copy(d).wait_recv()
            lag(d)

    en1.wait_send()
    en2.wait_send()
    pair.wait_send()

    @pl.loop(0, CHUNKS)
    def _(i):
        bulk(i).wait_send()

    @pl.when(late)
    def _():
        dl.wait_send()

    @pl.when(early)
    def _():
        for d in range(1, NX):
            x_copy(d).wait_send()
            xa_copy(d).wait_send()
        for d in range(1, NZ):
            z_copy(d).wait_send()
            za_copy(d).wait_send()
        for d in range(1, NY):
            y_copy(d).wait_send()
        for d in range(NX):
            fw_copy(d).wait_send()


def per_device(factors, occ_energy, vir_energy, pair_code, pair_count):
    _, V, A = factors.shape
    table = jnp.concatenate(
        [
            jnp.broadcast_to(vir_energy.astype(F32)[None, :], (8, V)),
            jnp.broadcast_to(occ_energy.astype(F32)[:, None], (8, V)),
        ]
    )
    dma = pltpu.SemaphoreType.DMA
    vmem, smem = pl.BlockSpec(memory_space=pltpu.VMEM), pl.BlockSpec(memory_space=pltpu.SMEM)
    rx, rz = V // NX, V // NX // NZ
    flops = 2 * V * V * A * 7
    aux, lag = pl.pallas_call(
        body,
        out_shape=[jax.ShapeDtypeStruct((V, A), BF16)] * 2,
        in_specs=[vmem, vmem, smem, smem],
        out_specs=[vmem, vmem],
        scratch_shapes=[
            pltpu.VMEM((2, V, A), BF16),
            pltpu.VMEM((3, V, V), BF16),
            pltpu.VMEM((2, 8, V), F32),
            pltpu.VMEM((V, V), F32),
            pltpu.VMEM((V, A), F32),
            pltpu.VMEM((V, V), F32),
            pltpu.VMEM((V, V), BF16),
            pltpu.VMEM((V, V), BF16),
            pltpu.VMEM((V, V), BF16),
            pltpu.VMEM((NX - 1, rx, V), BF16),
            pltpu.VMEM((rx, V), BF16),
            pltpu.VMEM((NZ - 1, rz, V), BF16),
            pltpu.VMEM((rz, V), BF16),
            pltpu.VMEM((NY - 1, rz, V), BF16),
            pltpu.VMEM((V, V), BF16),
            dma, dma, dma((CHUNKS,)), dma((CHUNKS,)), dma((2,)), dma((2,)), dma, dma,
            dma((NX - 1,)), dma((NX - 1,)), dma((NZ - 1,)), dma((NZ - 1,)), dma((NY - 1,)), dma((NY - 1,)),
            dma((NZ - 1,)), dma((NZ - 1,)), dma((NX - 1,)), dma((NX - 1,)), dma((NX,)), dma((NX,)),
        ],
        compiler_params=pltpu.CompilerParams(
            collective_id=0, has_side_effects=True, vmem_limit_bytes=36 * 2**20
        ),
        cost_estimate=pl.CostEstimate(flops=flops, bytes_accessed=8 * V * A, transcendentals=0),
        name="window",
    )(factors.reshape(V, A), table, pair_code, pair_count)
    return aux.reshape(1, V, A), lag.reshape(1, V, A)


def solution(mesh):
    in_specs = (
        P(("grp", "mem"), None, None),
        P(("grp", "mem")),
        P(),
        P("grp", None, None),
        P("grp", None),
    )
    out_specs = (P(("grp", "mem"), None, None), P(("grp", "mem"), None, None))
    return jax.shard_map(
        per_device, mesh=mesh, in_specs=in_specs, out_specs=out_specs, check_vma=False
    )
```

time: 301 us -> 83 us (0.28)
  waiting for transfers between devices: 130 us -> 0 us
  Pallas kernels: 0 us -> 75.2 us
  starting transfers between devices: 54.6 us -> 0 us
  blocking collectives: 44.8 us -> 0 us
  other arithmetic: 21.4 us -> 0 us
  matrix products: 14.2 us -> 0 us
  between operations: 14.8 us -> 1.3 us
  local copies, waits for them, and re-layouts: 17 us -> 6.33 us
  loops' own time: 3.39 us -> 0 us
    psum x1 -> x0, waiting for transfers between devices: 77.5 us -> none  [per_device(): density = lax.psum(density, 'grp')]
    pallas_call x0 -> x1, Pallas kernels: none -> 75.2 us  [per_device(): pl.pallas_call(body, out_shape=[jax.ShapeDtypeStruct((V, A), BF16)] * 2,...]
    all_to_all x1 -> x0, starting transfers between devices: 50.3 us -> none  [sum_at_owner(): lax.all_to_all(cut_along(value, dim, length), axis, 0, 0, tiled=True)]
    all_to_all x1 -> x0, blocking collectives: 44.8 us -> none  [from_everyone(): return lax.all_to_all(copies, axis, split_axis=0, concat_axis=0, tiled=True)]
    ppermute x6 -> x0, waiting for transfers between devices: 43.4 us -> none  [partner(): return lax.ppermute(value, axis, pairs)]
    dot_general x5 -> x0, matrix products: 14.2 us -> none  [the longest x1 6.01 us: pair_terms(): lax.dot_general(left_block, right_block, (((1,), (1,)), ((), ())), prefer...]
    another operation x2 -> x0, other arithmetic: 11 us -> none
    all_to_all x1 -> x0, waiting for transfers between devices: 9.28 us -> none  [sum_at_owner(): lax.all_to_all(cut_along(value, dim, length), axis, 0, 0, tiled=True)]
  transfers between devices with their start and end apart: 8 -> 0, of which waited for: 3 -> 0; matrix products, arithmetic and copies ran while one was open for 6% -> 0% of each run, Pallas kernels for 0% -> 0%
where the time goes in v1:
time: 83 us; the launch traced here: 82.8 us
  Pallas kernels  75.2 us (91%)
  local copies, waits for them, and re-layouts  6.33 us (8%)
  between operations  1.3 us (2%)
    pallas_call x1, Pallas kernels, per_device(): pl.pallas_call(body, out_shape=[jax.ShapeDtypeStruct((V, A), BF16)] * 2,...  75.2 us
    unnamed x7, local copies, waits for them, and re-layouts  5.65 us

profile of v1, /device:TPU:16, one launch (start us, length us, event | category | flops | bytes accessed | tf_op | source)
XLA Modules:
  0.0 82.8 jit_solution(2409437972883630169)
XLA Ops:
  1.3 0.7 broadcast_in_dim.7
  2.0 0.8 copy.7.code
  2.7 0.0 copy-start
  2.7 1.6 %copy-done = bf16[1,512,2048]{2,1,0:T(8,128)(2,1)S(1)} copy-done((bf16[1,512,2048]{2,1,0:T(8,128)(2,1)S(1)}, bf16[1,512,2048]{2,1,0:T(8,128)(2,1)}, u32[]{:S(2)}) %copy-start) | copy-done | bytes 2097176
  4.3 0.0 copy-start.1
  4.3 0.7 copy-done.1
  5.0 75.2 %window.1 = (bf16[512,2048]{1,0:T(8,128)(2,1)S(1)}, bf16[512,2048]{1,0:T(8,128)(2,1)S(1)}) custom-call(bf16[512,2048]{1,0:T(8,128)(2,1)S(1)} %bitcast.8, f32[16,512]{1,0:T(8,128)S(1)} %concatenate.3.table, s32[1,32,3]{2,1,0:T(8,128)S(1)} %copy.7.code, s32[1,32]{1,0:T(1,128)S(1)} %copy-done.1), custom_call_target="tpu_custom_call" | custom-call | flops 7516192768 | bytes 8388608 | tf_op jit(solution)/shard_map/window/pallas_call | solution.py:362
  80.2 1.3 %copy.11 = bf16[1,512,2048]{2,1,0:T(8,128)(2,1)} copy(bf16[1,512,2048]{2,1,0:T(8,128)(2,1)S(1)} %bitcast.7) | data formatting | bytes 4194304
  81.5 1.3 %copy.12 = bf16[1,512,2048]{2,1,0:T(8,128)(2,1)} copy(bf16[1,512,2048]{2,1,0:T(8,128)(2,1)S(1)} %bitcast.6) | data formatting | bytes 4194304
  (1 shorter events, 0.0 us)
Async XLA Ops:
  2.7 1.6 %copy-start = (bf16[1,512,2048]{2,1,0:T(8,128)(2,1)S(1)}, bf16[1,512,2048]{2,1,0:T(8,128)(2,1)}, u32[]{:S(2)}) copy-start(bf16[1,512,2048]{2,1,0:T(8,128)(2,1)} %param.5) | copy-start | bytes 6291460
  4.3 0.7 copy-start.1

commit v2 on v1

--- a/solution.py
+++ b/solution.py
@@ -12,6 +12,11 @@
 CHUNKS = 16
 FIRST = 7
 LEAD = 2
+LAST = 384
+FAR_FIRST = sorted(
+    range(1, NX * NZ),
+    key=lambda d: (-min(d // NZ, NX - d // NZ) - min(d % NZ, NZ - d % NZ), d),
+)
 F32, BF16 = jnp.float32, jnp.bfloat16
 
 
@@ -28,13 +33,13 @@
 
 
 def body(
-    b_own, table, code, count,
+    b_hbm, table, code, count,
     gamma_out, lag_out,
-    ball, tall, ens, vsum, acc, dens, dl_send, dl_recv, xs, xr, zs, zr, ys, yr, dfull,
-    pair_s, pair_r, bulk_s, bulk_r, en_s, en_r, dl_s, dl_rs,
-    x_s, x_r, z_s, z_r, y_s, y_r, za_s, za_r, xa_s, xa_r, fw_s, fw_r,
+    b_own, ball, tall, ens, vsum, acc, dens, dl_send, dl_recv, xs, pr, ys, yr, dfull,
+    load_sem, pair_s, pair_r, bulk_s, bulk_r, en_s, en_r, dl_s, dl_rs,
+    p_s, p_r, y_s, y_r, f_s, f_r, fw_s, fw_r,
 ):
-    V, A = b_own.shape
+    V, A = b_hbm.shape
     g, m = lax.axis_index("grp"), lax.axis_index("mem")
     x, ylo = lax.rem(g, NX), g // NX
     core, yhi, z = lax.rem(m, 2), lax.rem(m // 2, 2), m // 4
@@ -45,11 +50,15 @@
     late = core != yhi
     rows_x, rows_z = V // NX, V // NX // NZ
 
-    def to_x(d):
-        return {"grp": ylo * NX + lax.rem(x + d, NX), "mem": m}
-
-    def to_z(d):
-        return {"grp": g, "mem": lax.rem(z + d, NZ) * 4 + yhi * 2 + core}
+    load = pltpu.make_async_copy(b_hbm, b_own, load_sem)
+    load.start()
+
+    def to_plane(d):
+        dx, dz = d // NZ, d % NZ
+        return {
+            "grp": ylo * NX + lax.rem(x + dx, NX),
+            "mem": lax.rem(z + dz, NZ) * 4 + yhi * 2 + core,
+        }
 
     def to_y(d):
         other = lax.rem(y + d, NY)
@@ -74,10 +83,8 @@
 
     @pl.when(early)
     def _():
-        for d in range(1, NX):
-            greet(to_x(d))
-        for d in range(1, NZ):
-            greet(to_z(d))
+        for d in FAR_FIRST:
+            greet(to_plane(d))
         for d in range(1, NY):
             greet(to_y(d))
 
@@ -107,10 +114,11 @@
 
     @pl.when(early)
     def _():
-        pl.semaphore_wait(barrier, 2 + NX - 1 + NZ - 1 + NY - 1)
+        pl.semaphore_wait(barrier, 2 + NX * NZ - 1 + NY - 1)
 
     en1.start()
     en2.start()
+    load.wait()
 
     @pl.when(late)
     def _():
@@ -120,8 +128,8 @@
 
     def lives(who, rnd):
         total = jnp.int32(0)
-        for s in range(code.shape[2]):
-            hit = jnp.logical_and(code[0, who, s] == rnd, s < count[0, who])
+        for s in range(code.shape[0]):
+            hit = jnp.logical_and(code[s, 0, who] == rnd, s < count[0, who])
             total = total + jnp.where(hit, 1, 0)
         return total.astype(F32)
 
@@ -206,6 +214,19 @@
         outer(2, 256, 128, c2)
 
     gamma(2, 256, 128, w2)
+    @pl.when(early)
+    def _():
+        dl.wait_recv()
+
+        @pl.loop(0, V // 256)
+        def _(p):
+            c = pl.ds(pl.multiple_of(p * 256, 256), 256)
+            dens[:, c] = dens[:, c] + dl_recv[:, c].astype(F32)
+
+        for lo in (0, 128, 256):
+            rows = slice(lo, lo + 128)
+            dens[rows, 0:LAST] = dens[rows, 0:LAST] + d2 * tn(tall[2, :, rows], tall[2, :, 0:LAST])
+
     bulk_wait(3 * CHUNKS // 4, CHUNKS - LEAD)
 
     @pl.when(early)
@@ -213,113 +234,96 @@
         bulk_start(0, FIRST)
 
     bulk_wait(CHUNKS - LEAD, CHUNKS)
-    tile(2, 384, 128, far_energy)
+    tile(2, LAST, 128, far_energy)
+
+    def piece(d):
+        dx, dz = d // NZ, d % NZ
+        return pl.ds(
+            pl.multiple_of(lax.rem(x + dx, NX) * rows_x + lax.rem(z + dz, NZ) * rows_z, rows_z), rows_z
+        )
+
+    def back(d):
+        dx, dz = d // NZ, d % NZ
+        return ((NX - dx) % NX) * NZ + (NZ - dz) % NZ
 
     def block_x(d):
         return pl.ds(pl.multiple_of(lax.rem(x + d, NX) * rows_x, rows_x), rows_x)
 
-    def block_z(d):
-        return pl.ds(pl.multiple_of(lax.rem(z + d, NZ) * rows_z, rows_z), rows_z)
-
-    def piece(d):
-        return pl.ds(pl.multiple_of(x * rows_x + lax.rem(z + d, NZ) * rows_z, rows_z), rows_z)
-
-    x_order = (1, 3, 2)
-    z_order = (4, 3, 5, 2, 6, 1, 7)
-
-    @pl.when(early)
-    def _():
-        outer(2, 384, 128, c2)
-        inner(2, d2)
-        dl.wait_recv()
-        dens[...] = dens[...] + dl_recv[...].astype(F32)
-        xs[...] = dens[...].astype(BF16)
-        for d in x_order:
-            remote(xs.at[block_x(d)], xr.at[d - 1], x_s.at[d - 1], x_r.at[d - 1], to_x(d)).start()
-
-    gamma(2, 384, 128, w2)
-    gamma_out[...] = acc[...].astype(BF16)
-
-    def x_copy(d):
-        return remote(xs.at[block_x(d)], xr.at[d - 1], x_s.at[d - 1], x_r.at[d - 1], to_x(d))
-
-    def z_copy(d):
-        return remote(zs.at[block_z(d)], zr.at[d - 1], z_s.at[d - 1], z_r.at[d - 1], to_z(d))
+    def part_copy(d):
+        return remote(xs.at[piece(d)], pr.at[d - 1], p_s.at[d - 1], p_r.at[d - 1], to_plane(d))
 
     def y_copy(d):
         return remote(ys, yr.at[d - 1], y_s.at[d - 1], y_r.at[d - 1], to_y(d))
 
-    def za_copy(d):
-        return remote(dfull.at[piece(0)], dfull.at[piece(0)], za_s.at[d - 1], za_r.at[d - 1], to_z(d))
-
-    def za_arrival(d):
-        r = piece(NZ - d)
-        return remote(dfull.at[r], dfull.at[r], za_s.at[d - 1], za_r.at[d - 1], to_z(d))
-
-    def xa_copy(d):
-        r = block_x(0)
-        return remote(dfull.at[r], dfull.at[r], xa_s.at[d - 1], xa_r.at[d - 1], to_x(d))
-
-    def xa_arrival(d):
-        r = block_x(NX - d)
-        return remote(dfull.at[r], dfull.at[r], xa_s.at[d - 1], xa_r.at[d - 1], to_x(d))
+    def full_copy(d):
+        r = piece(0)
+        return remote(dfull.at[r], dfull.at[r], f_s.at[d - 1], f_r.at[d - 1], to_plane(d))
+
+    def full_arrival(d):
+        r = piece(back(d))
+        return remote(dfull.at[r], dfull.at[r], f_s.at[d - 1], f_r.at[d - 1], to_plane(d))
 
     def fw_copy(d):
-        r = block_x(lax.rem(NX - d, NX))
+        r = block_x((NX - d) % NX)
         return remote(dfull.at[r], dfull.at[r], fw_s.at[d], fw_r.at[d], to_mate)
 
     def lag(d):
-        r = block_x(lax.rem(NX - d, NX))
+        r = block_x((NX - d) % NX)
 
         @pl.loop(0, A // 512)
         def _(p):
             c = pl.ds(pl.multiple_of(p * 512, 512), 512)
             lag_out[r, c] = nn(dfull[r, :], b_own[:, c]).astype(BF16)
 
-    @pl.when(early)
-    def _():
-        for d in x_order:
-            x_copy(d).wait_recv()
-        sum_x = dens[block_x(0), :]
-        for d in range(NX - 1):
-            sum_x = sum_x + xr[d].astype(F32)
-        dens[0:rows_x, :] = sum_x
-        zs[...] = sum_x.astype(BF16)
-        for d in z_order:
-            z_copy(d).start()
-        for d in z_order:
-            z_copy(d).wait_recv()
-        sum_z = dens[block_z(0), :]
-        for d in range(NZ - 1):
-            sum_z = sum_z + zr[d].astype(F32)
-        ys[...] = sum_z.astype(BF16)
+    x_order = (0, 1, 3, 2)
+
+    @pl.when(early)
+    def _():
+        new = tall[2, :, LAST:V]
+        dens[0:LAST, LAST:V] = dens[0:LAST, LAST:V] + d2 * tn(tall[2, :, 0:LAST], new)
+        dens[LAST:V, :] = dens[LAST:V, :] + d2 * tn(new, tall[2])
+
+        @pl.loop(0, V // 256)
+        def _(p):
+            c = pl.ds(pl.multiple_of(p * 256, 256), 256)
+            total = dens[:, c] + c2 * nt(new, tall[2, c, LAST:V])
+            dens[:, c] = total
+            xs[:, c] = total.astype(BF16)
+
+        for d in FAR_FIRST:
+            part_copy(d).start()
+
+    gamma(2, LAST, 128, w2)
+    gamma_out[...] = acc[...].astype(BF16)
+
+    @pl.when(early)
+    def _():
+        total = dens[piece(0), :]
+        for d in FAR_FIRST[::-1]:
+            part_copy(d).wait_recv()
+            total = total + pr[d - 1].astype(F32)
+        ys[...] = total.astype(BF16)
         for d in (2, 1, 3):
             y_copy(d).start()
         bulk_start(FIRST, CHUNKS)
-        for d in (2, 1, 3):
+        for d in (1, 3, 2):
             y_copy(d).wait_recv()
-        total = sum_z
-        for d in range(NY - 1):
-            total = total + yr[d].astype(F32)
+            total = total + yr[d - 1].astype(F32)
         dfull[piece(0), :] = (total * (1.0 / (8.0 * 2 * NX * NY * NZ))).astype(BF16)
-        for d in z_order:
-            za_copy(d).start()
-        for d in z_order:
-            za_arrival(d).wait_recv()
-        for d in x_order:
-            xa_copy(d).start()
-        fw_copy(0).start()
-        lag(0)
-        for d in x_order:
-            xa_arrival(d).wait_recv()
-            fw_copy(d).start()
-            lag(d)
+        for d in FAR_FIRST:
+            full_copy(d).start()
+        for dx in x_order:
+            for dz in (0, 1, 7, 2, 6, 3, 5, 4):
+                if dx or dz:
+                    full_arrival(dx * NZ + dz).wait_recv()
+            fw_copy(dx).start()
+            lag(dx)
 
     @pl.when(late)
     def _():
-        for d in (0,) + x_order:
-            fw_copy(d).wait_recv()
-            lag(d)
+        for dx in x_order:
+            fw_copy(dx).wait_recv()
+            lag(dx)
 
     en1.wait_send()
     en2.wait_send()
@@ -335,12 +339,9 @@
 
     @pl.when(early)
     def _():
-        for d in range(1, NX):
-            x_copy(d).wait_send()
-            xa_copy(d).wait_send()
-        for d in range(1, NZ):
-            z_copy(d).wait_send()
-            za_copy(d).wait_send()
+        for d in range(1, NX * NZ):
+            part_copy(d).wait_send()
+            full_copy(d).wait_send()
         for d in range(1, NY):
             y_copy(d).wait_send()
         for d in range(NX):
@@ -357,14 +358,15 @@
     )
     dma = pltpu.SemaphoreType.DMA
     vmem, smem = pl.BlockSpec(memory_space=pltpu.VMEM), pl.BlockSpec(memory_space=pltpu.SMEM)
-    rx, rz = V // NX, V // NX // NZ
+    rz, plane = V // NX // NZ, NX * NZ - 1
     flops = 2 * V * V * A * 7
     aux, lag = pl.pallas_call(
         body,
         out_shape=[jax.ShapeDtypeStruct((V, A), BF16)] * 2,
-        in_specs=[vmem, vmem, smem, smem],
+        in_specs=[pl.BlockSpec(memory_space=pltpu.HBM), vmem, smem, smem],
         out_specs=[vmem, vmem],
         scratch_shapes=[
+            pltpu.VMEM((V, A), BF16),
             pltpu.VMEM((2, V, A), BF16),
             pltpu.VMEM((3, V, V), BF16),
             pltpu.VMEM((2, 8, V), F32),
@@ -374,22 +376,25 @@
             pltpu.VMEM((V, V), BF16),
             pltpu.VMEM((V, V), BF16),
             pltpu.VMEM((V, V), BF16),
-            pltpu.VMEM((NX - 1, rx, V), BF16),
-            pltpu.VMEM((rx, V), BF16),
-            pltpu.VMEM((NZ - 1, rz, V), BF16),
+            pltpu.VMEM((plane, rz, V), BF16),
             pltpu.VMEM((rz, V), BF16),
             pltpu.VMEM((NY - 1, rz, V), BF16),
             pltpu.VMEM((V, V), BF16),
-            dma, dma, dma((CHUNKS,)), dma((CHUNKS,)), dma((2,)), dma((2,)), dma, dma,
-            dma((NX - 1,)), dma((NX - 1,)), dma((NZ - 1,)), dma((NZ - 1,)), dma((NY - 1,)), dma((NY - 1,)),
-            dma((NZ - 1,)), dma((NZ - 1,)), dma((NX - 1,)), dma((NX - 1,)), dma((NX,)), dma((NX,)),
+            dma, dma, dma, dma((CHUNKS,)), dma((CHUNKS,)), dma((2,)), dma((2,)), dma, dma,
+            dma((plane,)), dma((plane,)), dma((NY - 1,)), dma((NY - 1,)),
+            dma((plane,)), dma((plane,)), dma((NX,)), dma((NX,)),
         ],
         compiler_params=pltpu.CompilerParams(
             collective_id=0, has_side_effects=True, vmem_limit_bytes=36 * 2**20
         ),
         cost_estimate=pl.CostEstimate(flops=flops, bytes_accessed=8 * V * A, transcendentals=0),
         name="window",
-    )(factors.reshape(V, A), table, pair_code, pair_count)
+    )(
+        pltpu.with_memory_space_constraint(factors.reshape(V, A), pltpu.HBM),
+        table,
+        pltpu.with_memory_space_constraint(jnp.transpose(pair_code, (2, 0, 1)), pltpu.HBM),
+        pltpu.with_memory_space_constraint(pair_count, pltpu.HBM),
+    )
     return aux.reshape(1, V, A), lag.reshape(1, V, A)
 
 

time: 83 us -> 74.5 us (0.90)
  Pallas kernels: 75.2 us -> 69.7 us
  local copies, waits for them, and re-layouts: 6.33 us -> 3.33 us
    pallas_call x1, Pallas kernels: 75.2 us -> 69.7 us  [per_device(): pl.pallas_call(body, out_shape=[jax.ShapeDtypeStruct((V, A), BF16)] * 2,...]
    unnamed x7 -> x2, local copies, waits for them, and re-layouts: 5.65 us -> 2.64 us
where the time goes in v2:
time: 74.5 us; the launch traced here: 74.3 us
  Pallas kernels  69.7 us (94%)
  local copies, waits for them, and re-layouts  3.33 us (4%)
  between operations  1.29 us (2%)
    pallas_call x1, Pallas kernels, per_device(): pl.pallas_call(body, out_shape=[jax.ShapeDtypeStruct((V, A), BF16)] * 2,...  69.7 us
    unnamed x2, local copies, waits for them, and re-layouts  2.64 us

profile of v2, /device:TPU:16, one launch (start us, length us, event | category | flops | bytes accessed | tf_op | source)
XLA Modules:
  0.0 74.3 jit_solution(7772301766892543632)
XLA Ops:
  1.3 0.7 broadcast_in_dim.7
  2.0 69.7 %window.1 = (bf16[512,2048]{1,0:T(8,128)(2,1)S(1)}, bf16[512,2048]{1,0:T(8,128)(2,1)S(1)}) custom-call(bf16[512,2048]{1,0:T(8,128)(2,1)} %bitcast.9, f32[16,512]{1,0:T(8,128)S(1)} %concatenate.3.table, s32[3,1,32]{2,1,0:T(1,128)} %bitcast.10, s32[1,32]{1,0:T(1,128)} %count.1), custom_call_target="tpu_custom_call" | custom-call | flops 7516192768 | bytes 8388608 | tf_op jit(solution)/shard_map/window/pallas_call | solution.py:363
  71.7 1.3 %copy.10 = bf16[1,512,2048]{2,1,0:T(8,128)(2,1)} copy(bf16[1,512,2048]{2,1,0:T(8,128)(2,1)S(1)} %bitcast.8) | data formatting | bytes 4194304
  73.0 1.3 %copy.11 = bf16[1,512,2048]{2,1,0:T(8,128)(2,1)} copy(bf16[1,512,2048]{2,1,0:T(8,128)(2,1)S(1)} %bitcast.7) | data formatting | bytes 4194304
  (1 shorter events, 0.0 us)

commit v3 on v2

--- a/solution.py
+++ b/solution.py
@@ -10,9 +10,9 @@
 MESH = pl.DeviceIdType.MESH
 NX, NY, NZ = 4, 4, 8
 CHUNKS = 16
-FIRST = 7
-LEAD = 2
+LEAD = 1
 LAST = 384
+STEPS = 4
 FAR_FIRST = sorted(
     range(1, NX * NZ),
     key=lambda d: (-min(d // NZ, NX - d // NZ) - min(d % NZ, NZ - d % NZ), d),
@@ -34,10 +34,10 @@
 
 def body(
     b_hbm, table, code, count,
-    gamma_out, lag_out,
-    b_own, ball, tall, ens, vsum, acc, dens, dl_send, dl_recv, xs, pr, ys, yr, dfull,
+    gamma_out, dfull,
+    b_own, ball, tall, ens, vsum, acc, dens, dl_send, dl_recv, xs, pr, ys, yr,
     load_sem, pair_s, pair_r, bulk_s, bulk_r, en_s, en_r, dl_s, dl_rs,
-    p_s, p_r, y_s, y_r, f_s, f_r, fw_s, fw_r,
+    p_s, p_r, y_s, y_r, f_s, f_r, fw_s, fw_r, go,
 ):
     V, A = b_hbm.shape
     g, m = lax.axis_index("grp"), lax.axis_index("mem")
@@ -57,10 +57,22 @@
         dx, dz = d // NZ, d % NZ
         return {
             "grp": ylo * NX + lax.rem(x + dx, NX),
-            "mem": lax.rem(z + dz, NZ) * 4 + yhi * 2 + core,
+            "mem": lax.rem(z + dz, NZ) * 4 + yhi * 2 + 1 - yhi,
         }
 
-    def to_y(d):
+    def to_plane_early(d):
+        dx, dz = d // NZ, d % NZ
+        return {
+            "grp": ylo * NX + lax.rem(x + dx, NX),
+            "mem": lax.rem(z + dz, NZ) * 4 + yhi * 2 + yhi,
+        }
+
+    def late_y(d):
+        other = lax.rem(y + d, NY)
+        hi, lo = other // 2, lax.rem(other, 2)
+        return {"grp": lo * NX + x, "mem": z * 4 + hi * 2 + 1 - hi}
+
+    def early_y(d):
         other = lax.rem(y + d, NY)
         hi, lo = other // 2, lax.rem(other, 2)
         return {"grp": lo * NX + x, "mem": z * 4 + hi * 3}
@@ -81,12 +93,12 @@
     greet(to_mate)
     greet(to_far)
 
-    @pl.when(early)
+    @pl.when(late)
     def _():
         for d in FAR_FIRST:
-            greet(to_plane(d))
+            greet(to_plane_early(d))
         for d in range(1, NY):
-            greet(to_y(d))
+            greet(early_y(d))
 
     crows = V // CHUNKS
 
@@ -115,6 +127,10 @@
     @pl.when(early)
     def _():
         pl.semaphore_wait(barrier, 2 + NX * NZ - 1 + NY - 1)
+
+    @pl.when(early)
+    def _():
+        pl.semaphore_signal(go, inc=1, device_id=to_mate, device_id_type=MESH)
 
     en1.start()
     en2.start()
@@ -198,24 +214,18 @@
     w2 = c2 + d2
     far_energy = ens[1, 0:1, 0:1]
 
-    bulk_wait(0, CHUNKS // 2)
-    tile(2, 0, 256, far_energy)
+    Q = CHUNKS // 4
 
     @pl.when(early)
     def _():
+        bulk_wait(0, 2 * Q)
+        tile(2, 0, 256, far_energy)
         outer(2, 0, 256, c2)
-
-    gamma(2, 0, 256, w2)
-    bulk_wait(CHUNKS // 2, 3 * CHUNKS // 4)
-    tile(2, 256, 128, far_energy)
-
-    @pl.when(early)
-    def _():
+        gamma(2, 0, 256, w2)
+        bulk_wait(2 * Q, 3 * Q)
+        tile(2, 256, 128, far_energy)
         outer(2, 256, 128, c2)
-
-    gamma(2, 256, 128, w2)
-    @pl.when(early)
-    def _():
+        gamma(2, 256, 128, w2)
         dl.wait_recv()
 
         @pl.loop(0, V // 256)
@@ -227,14 +237,10 @@
             rows = slice(lo, lo + 128)
             dens[rows, 0:LAST] = dens[rows, 0:LAST] + d2 * tn(tall[2, :, rows], tall[2, :, 0:LAST])
 
-    bulk_wait(3 * CHUNKS // 4, CHUNKS - LEAD)
-
-    @pl.when(early)
-    def _():
-        bulk_start(0, FIRST)
-
-    bulk_wait(CHUNKS - LEAD, CHUNKS)
-    tile(2, LAST, 128, far_energy)
+        bulk_wait(3 * Q, CHUNKS - LEAD)
+        bulk_start(0, CHUNKS)
+        bulk_wait(CHUNKS - LEAD, CHUNKS)
+        tile(2, LAST, 128, far_energy)
 
     def piece(d):
         dx, dz = d // NZ, d % NZ
@@ -250,10 +256,10 @@
         return pl.ds(pl.multiple_of(lax.rem(x + d, NX) * rows_x, rows_x), rows_x)
 
     def part_copy(d):
-        return remote(xs.at[piece(d)], pr.at[d - 1], p_s.at[d - 1], p_r.at[d - 1], to_plane(d))
+        return remote(xs.at[piece(d)], pr.at[d], p_s.at[d], p_r.at[d], to_plane(d))
 
     def y_copy(d):
-        return remote(ys, yr.at[d - 1], y_s.at[d - 1], y_r.at[d - 1], to_y(d))
+        return remote(ys, yr.at[d - 1], y_s.at[d - 1], y_r.at[d - 1], late_y(d))
 
     def full_copy(d):
         r = piece(0)
@@ -267,14 +273,6 @@
         r = block_x((NX - d) % NX)
         return remote(dfull.at[r], dfull.at[r], fw_s.at[d], fw_r.at[d], to_mate)
 
-    def lag(d):
-        r = block_x((NX - d) % NX)
-
-        @pl.loop(0, A // 512)
-        def _(p):
-            c = pl.ds(pl.multiple_of(p * 512, 512), 512)
-            lag_out[r, c] = nn(dfull[r, :], b_own[:, c]).astype(BF16)
-
     x_order = (0, 1, 3, 2)
 
     @pl.when(early)
@@ -286,44 +284,47 @@
         @pl.loop(0, V // 256)
         def _(p):
             c = pl.ds(pl.multiple_of(p * 256, 256), 256)
-            total = dens[:, c] + c2 * nt(new, tall[2, c, LAST:V])
-            dens[:, c] = total
-            xs[:, c] = total.astype(BF16)
-
-        for d in FAR_FIRST:
+            xs[:, c] = (dens[:, c] + c2 * nt(new, tall[2, c, LAST:V])).astype(BF16)
+
+        for d in FAR_FIRST + [0]:
             part_copy(d).start()
-
-    gamma(2, LAST, 128, w2)
-    gamma_out[...] = acc[...].astype(BF16)
-
-    @pl.when(early)
-    def _():
-        total = dens[piece(0), :]
-        for d in FAR_FIRST[::-1]:
+        gamma(2, LAST, 128, w2)
+        gamma_out[...] = acc[...].astype(BF16)
+        for dx in x_order:
+            fw_copy(dx).wait_recv()
+
+    @pl.when(late)
+    def _():
+        bulk_wait(0, Q)
+        tile(2, 0, 128, far_energy)
+        pl.semaphore_wait(go, 1)
+        total = jnp.zeros((rows_z, V), F32)
+        for d in [0] + FAR_FIRST[::-1]:
             part_copy(d).wait_recv()
-            total = total + pr[d - 1].astype(F32)
+            total = total + pr[d].astype(F32)
         ys[...] = total.astype(BF16)
         for d in (2, 1, 3):
             y_copy(d).start()
-        bulk_start(FIRST, CHUNKS)
         for d in (1, 3, 2):
             y_copy(d).wait_recv()
             total = total + yr[d - 1].astype(F32)
         dfull[piece(0), :] = (total * (1.0 / (8.0 * 2 * NX * NY * NZ))).astype(BF16)
         for d in FAR_FIRST:
             full_copy(d).start()
+        bulk_wait(Q, 2 * Q)
+        tile(2, 128, 128, far_energy)
+        bulk_wait(2 * Q, 3 * Q)
+        tile(2, 256, 128, far_energy)
+        gamma(2, 0, LAST, w2)
+        bulk_wait(3 * Q, CHUNKS)
+        tile(2, LAST, 128, far_energy)
+        gamma(2, LAST, 128, w2)
+        gamma_out[...] = acc[...].astype(BF16)
         for dx in x_order:
             for dz in (0, 1, 7, 2, 6, 3, 5, 4):
                 if dx or dz:
                     full_arrival(dx * NZ + dz).wait_recv()
             fw_copy(dx).start()
-            lag(dx)
-
-    @pl.when(late)
-    def _():
-        for dx in x_order:
-            fw_copy(dx).wait_recv()
-            lag(dx)
 
     en1.wait_send()
     en2.wait_send()
@@ -336,16 +337,40 @@
     @pl.when(late)
     def _():
         dl.wait_send()
-
-    @pl.when(early)
-    def _():
-        for d in range(1, NX * NZ):
-            part_copy(d).wait_send()
-            full_copy(d).wait_send()
         for d in range(1, NY):
             y_copy(d).wait_send()
+        for d in range(1, NX * NZ):
+            full_copy(d).wait_send()
         for d in range(NX):
             fw_copy(d).wait_send()
+
+    @pl.when(early)
+    def _():
+        for d in range(NX * NZ):
+            part_copy(d).wait_send()
+
+
+def finish(b, d, g, aux, lag, stage, aux_sem, lag_sem):
+    out = pltpu.make_async_copy(g, aux, aux_sem)
+    out.start()
+    A = b.shape[1]
+    width = A // lag_sem.shape[0]
+
+    def copy(p):
+        c = pl.ds(pl.multiple_of(p * width, 128), width)
+        return pltpu.make_async_copy(stage.at[:, c], lag.at[:, c], lag_sem.at[p])
+
+    @pl.loop(0, A // width)
+    def _(p):
+        c = pl.ds(pl.multiple_of(p * width, 128), width)
+        stage[:, c] = nn(d[...], b[:, c]).astype(BF16)
+        copy(p).start()
+
+    @pl.loop(0, A // width)
+    def _(p):
+        copy(p).wait()
+
+    out.wait()
 
 
 def per_device(factors, occ_energy, vir_energy, pair_code, pair_count):
@@ -360,9 +385,9 @@
     vmem, smem = pl.BlockSpec(memory_space=pltpu.VMEM), pl.BlockSpec(memory_space=pltpu.SMEM)
     rz, plane = V // NX // NZ, NX * NZ - 1
     flops = 2 * V * V * A * 7
-    aux, lag = pl.pallas_call(
+    gamma, density = pl.pallas_call(
         body,
-        out_shape=[jax.ShapeDtypeStruct((V, A), BF16)] * 2,
+        out_shape=[jax.ShapeDtypeStruct((V, A), BF16), jax.ShapeDtypeStruct((V, V), BF16)],
         in_specs=[pl.BlockSpec(memory_space=pltpu.HBM), vmem, smem, smem],
         out_specs=[vmem, vmem],
         scratch_shapes=[
@@ -376,13 +401,13 @@
             pltpu.VMEM((V, V), BF16),
             pltpu.VMEM((V, V), BF16),
             pltpu.VMEM((V, V), BF16),
-            pltpu.VMEM((plane, rz, V), BF16),
+            pltpu.VMEM((NX * NZ, rz, V), BF16),
             pltpu.VMEM((rz, V), BF16),
             pltpu.VMEM((NY - 1, rz, V), BF16),
-            pltpu.VMEM((V, V), BF16),
             dma, dma, dma, dma((CHUNKS,)), dma((CHUNKS,)), dma((2,)), dma((2,)), dma, dma,
-            dma((plane,)), dma((plane,)), dma((NY - 1,)), dma((NY - 1,)),
+            dma((NX * NZ,)), dma((NX * NZ,)), dma((NY - 1,)), dma((NY - 1,)),
             dma((plane,)), dma((plane,)), dma((NX,)), dma((NX,)),
+            pltpu.SemaphoreType.REGULAR,
         ],
         compiler_params=pltpu.CompilerParams(
             collective_id=0, has_side_effects=True, vmem_limit_bytes=36 * 2**20
@@ -395,6 +420,17 @@
         pltpu.with_memory_space_constraint(jnp.transpose(pair_code, (2, 0, 1)), pltpu.HBM),
         pltpu.with_memory_space_constraint(pair_count, pltpu.HBM),
     )
+    anywhere = pl.BlockSpec(memory_space=pltpu.HBM)
+    aux, lag = pl.pallas_call(
+        finish,
+        out_shape=[jax.ShapeDtypeStruct((V, A), BF16)] * 2,
+        in_specs=[vmem, vmem, vmem],
+        out_specs=[anywhere, anywhere],
+        scratch_shapes=[pltpu.VMEM((V, A), BF16), dma, dma((STEPS,))],
+        compiler_params=pltpu.CompilerParams(vmem_limit_bytes=16 * 2**20),
+        cost_estimate=pl.CostEstimate(flops=2 * V * V * A, bytes_accessed=8 * V * A, transcendentals=0),
+        name="finish",
+    )(factors.reshape(V, A), density, gamma)
     return aux.reshape(1, V, A), lag.reshape(1, V, A)
 
 

time: 74.5 us -> 68.9 us (0.925)
  the two profiles are of different devices: /device:TPU:16 before, /device:TPU:33 now
where the time goes in v3:
time: 68.9 us; the launch traced here: 68.7 us
  Pallas kernels  66.7 us (97%)
  between operations  1.3 us (2%)
  local copies, waits for them, and re-layouts  0.69 us (1%)
    pallas_call x1, Pallas kernels, per_device(): pl.pallas_call(body, out_shape=[jax.ShapeDtypeStruct((V, A), BF16), jax.S...  64.1 us
    pallas_call x1, Pallas kernels, per_device(): pl.pallas_call(finish, out_shape=[jax.ShapeDtypeStruct((V, A), BF16)] * 2...  2.62 us

profile of v3, /device:TPU:33, one launch (start us, length us, event | category | flops | bytes accessed | tf_op | source)
XLA Modules:
  0.0 68.7 jit_solution(13819907619905244120)
XLA Ops:
  1.3 0.7 broadcast_in_dim.7
  2.0 0.0 copy-start
  2.0 64.1 %window.1 = (bf16[512,2048]{1,0:T(8,128)(2,1)S(1)}, bf16[512,512]{1,0:T(8,128)(2,1)S(1)}) custom-call(bf16[512,2048]{1,0:T(8,128)(2,1)} %bitcast.7, f32[16,512]{1,0:T(8,128)S(1)} %concatenate.3.table, s32[3,1,32]{2,1,0:T(1,128)} %bitcast.11, s32[1,32]{1,0:T(1,128)} %count.1), custom_call_target="tpu_custom_call" | custom-call | flops 7516192768 | bytes 8388608 | tf_op jit(solution)/shard_map/window/pallas_call | solution.py:388
  66.1 0.0 copy-done
  66.1 2.6 %finish.1 = (bf16[512,2048]{1,0:T(8,128)(2,1)}, bf16[512,2048]{1,0:T(8,128)(2,1)}) custom-call(bf16[512,2048]{1,0:T(8,128)(2,1)S(1)} %bitcast.8, bf16[512,512]{1,0:T(8,128)(2,1)S(1)} %get-tuple-element.6.d, bf16[512,2048]{1,0:T(8,128)(2,1)S(1)} %get-tuple-element.7.g), custom_call_target="tpu_custom_call" | custom-call | flops 1073741824 | bytes 8388608 | tf_op jit(solution)/shard_map/finish/pallas_call | solution.py:424
  (1 shorter events, 0.0 us)
Async XLA Ops:
  2.0 64.1 %copy-start = (bf16[1,512,2048]{2,1,0:T(8,128)(2,1)S(1)}, bf16[1,512,2048]{2,1,0:T(8,128)(2,1)}, u32[]{:S(2)}) copy-start(bf16[1,512,2048]{2,1,0:T(8,128)(2,1)} %param.5) | copy-start | bytes 6291460

commit v4 on v3

--- a/solution.py
+++ b/solution.py
@@ -11,6 +11,7 @@
 NX, NY, NZ = 4, 4, 8
 CHUNKS = 16
 LEAD = 1
+FIRST = 4
 LAST = 384
 STEPS = 4
 FAR_FIRST = sorted(
@@ -176,6 +177,14 @@
             c = pl.ds(pl.multiple_of(p * 256, 256), 256)
             acc[:, c] = acc[:, c] + weight * nn(tall[r, :, rows], blocks[r][rows, c])
 
+    def gamma_last(lo, width, weight):
+        rows = pl.ds(pl.multiple_of(lo, 128), width)
+
+        @pl.loop(0, A // 256)
+        def _(p):
+            c = pl.ds(pl.multiple_of(p * 256, 256), 256)
+            gamma_out[:, c] = (acc[:, c] + weight * nn(tall[2, :, rows], ball[1, rows, c])).astype(BF16)
+
     def outer(r, lo, width, weight):
         cols = pl.ds(pl.multiple_of(lo, 128), width)
 
@@ -238,7 +247,7 @@
             dens[rows, 0:LAST] = dens[rows, 0:LAST] + d2 * tn(tall[2, :, rows], tall[2, :, 0:LAST])
 
         bulk_wait(3 * Q, CHUNKS - LEAD)
-        bulk_start(0, CHUNKS)
+        bulk_start(0, FIRST)
         bulk_wait(CHUNKS - LEAD, CHUNKS)
         tile(2, LAST, 128, far_energy)
 
@@ -281,15 +290,19 @@
         dens[0:LAST, LAST:V] = dens[0:LAST, LAST:V] + d2 * tn(tall[2, :, 0:LAST], new)
         dens[LAST:V, :] = dens[LAST:V, :] + d2 * tn(new, tall[2])
 
-        @pl.loop(0, V // 256)
-        def _(p):
-            c = pl.ds(pl.multiple_of(p * 256, 256), 256)
-            xs[:, c] = (dens[:, c] + c2 * nt(new, tall[2, c, LAST:V])).astype(BF16)
+        for j in range(NX):
+            cols = slice(j * rows_x, (j + 1) * rows_x)
+            term = dens[:, cols] + c2 * nt(new, tall[2, cols, LAST:V])
+            for k in range(NX - 1):
+                i = (j - k) % NX
+                xs[i * rows_x : (i + 1) * rows_x, k * rows_x : (k + 1) * rows_x] = term[
+                    i * rows_x : (i + 1) * rows_x
+                ].astype(BF16)
 
         for d in FAR_FIRST + [0]:
             part_copy(d).start()
-        gamma(2, LAST, 128, w2)
-        gamma_out[...] = acc[...].astype(BF16)
+        bulk_start(FIRST, CHUNKS)
+        gamma_last(LAST, 128, w2)
         for dx in x_order:
             fw_copy(dx).wait_recv()
 
@@ -298,7 +311,7 @@
         bulk_wait(0, Q)
         tile(2, 0, 128, far_energy)
         pl.semaphore_wait(go, 1)
-        total = jnp.zeros((rows_z, V), F32)
+        total = jnp.zeros((rows_z, xs.shape[1]), F32)
         for d in [0] + FAR_FIRST[::-1]:
             part_copy(d).wait_recv()
             total = total + pr[d].astype(F32)
@@ -318,8 +331,7 @@
         gamma(2, 0, LAST, w2)
         bulk_wait(3 * Q, CHUNKS)
         tile(2, LAST, 128, far_energy)
-        gamma(2, LAST, 128, w2)
-        gamma_out[...] = acc[...].astype(BF16)
+        gamma_last(LAST, 128, w2)
         for dx in x_order:
             for dz in (0, 1, 7, 2, 6, 3, 5, 4):
                 if dx or dz:
@@ -350,7 +362,7 @@
             part_copy(d).wait_send()
 
 
-def finish(b, d, g, aux, lag, stage, aux_sem, lag_sem):
+def finish(b, d, g, aux, lag, full, stage, aux_sem, lag_sem):
     out = pltpu.make_async_copy(g, aux, aux_sem)
     out.start()
     A = b.shape[1]
@@ -360,10 +372,19 @@
         c = pl.ds(pl.multiple_of(p * width, 128), width)
         return pltpu.make_async_copy(stage.at[:, c], lag.at[:, c], lag_sem.at[p])
 
+    n = d.shape[0] // NX
+    for i in range(NX):
+        rows = slice(i * n, (i + 1) * n)
+        for k in range(NX - 1):
+            j = (i + k) % NX
+            full[rows, j * n : (j + 1) * n] = d[rows, k * n : (k + 1) * n]
+        j = (i + NX - 1) % NX
+        full[rows, j * n : (j + 1) * n] = d[j * n : (j + 1) * n, n : 2 * n].astype(F32).T.astype(BF16)
+
     @pl.loop(0, A // width)
     def _(p):
         c = pl.ds(pl.multiple_of(p * width, 128), width)
-        stage[:, c] = nn(d[...], b[:, c]).astype(BF16)
+        stage[:, c] = nn(full[...], b[:, c]).astype(BF16)
         copy(p).start()
 
     @pl.loop(0, A // width)
@@ -383,11 +404,12 @@
     )
     dma = pltpu.SemaphoreType.DMA
     vmem, smem = pl.BlockSpec(memory_space=pltpu.VMEM), pl.BlockSpec(memory_space=pltpu.SMEM)
+    W = V - V // NX
     rz, plane = V // NX // NZ, NX * NZ - 1
     flops = 2 * V * V * A * 7
     gamma, density = pl.pallas_call(
         body,
-        out_shape=[jax.ShapeDtypeStruct((V, A), BF16), jax.ShapeDtypeStruct((V, V), BF16)],
+        out_shape=[jax.ShapeDtypeStruct((V, A), BF16), jax.ShapeDtypeStruct((V, W), BF16)],
         in_specs=[pl.BlockSpec(memory_space=pltpu.HBM), vmem, smem, smem],
         out_specs=[vmem, vmem],
         scratch_shapes=[
@@ -400,10 +422,10 @@
             pltpu.VMEM((V, V), F32),
             pltpu.VMEM((V, V), BF16),
             pltpu.VMEM((V, V), BF16),
-            pltpu.VMEM((V, V), BF16),
-            pltpu.VMEM((NX * NZ, rz, V), BF16),
-            pltpu.VMEM((rz, V), BF16),
-            pltpu.VMEM((NY - 1, rz, V), BF16),
+            pltpu.VMEM((V, W), BF16),
+            pltpu.VMEM((NX * NZ, rz, W), BF16),
+            pltpu.VMEM((rz, W), BF16),
+            pltpu.VMEM((NY - 1, rz, W), BF16),
             dma, dma, dma, dma((CHUNKS,)), dma((CHUNKS,)), dma((2,)), dma((2,)), dma, dma,
             dma((NX * NZ,)), dma((NX * NZ,)), dma((NY - 1,)), dma((NY - 1,)),
             dma((plane,)), dma((plane,)), dma((NX,)), dma((NX,)),
@@ -426,7 +448,7 @@
         out_shape=[jax.ShapeDtypeStruct((V, A), BF16)] * 2,
         in_specs=[vmem, vmem, vmem],
         out_specs=[anywhere, anywhere],
-        scratch_shapes=[pltpu.VMEM((V, A), BF16), dma, dma((STEPS,))],
+        scratch_shapes=[pltpu.VMEM((V, V), BF16), pltpu.VMEM((V, A), BF16), dma, dma((STEPS,))],
         compiler_params=pltpu.CompilerParams(vmem_limit_bytes=16 * 2**20),
         cost_estimate=pl.CostEstimate(flops=2 * V * V * A, bytes_accessed=8 * V * A, transcendentals=0),
         name="finish",

time: 68.9 us -> 64.8 us (0.940)
  the two profiles are of different devices: /device:TPU:33 before, /device:TPU:16 now
where the time goes in v4:
time: 64.8 us; the launch traced here: 63.8 us
  Pallas kernels  61.8 us (95%)
  between operations  1.3 us (2%)
  local copies, waits for them, and re-layouts  0.69 us (1%)
    pallas_call x1, Pallas kernels, per_device(): pl.pallas_call(body, out_shape=[jax.ShapeDtypeStruct((V, A), BF16), jax.S...  59.1 us
    pallas_call x1, Pallas kernels, per_device(): pl.pallas_call(finish, out_shape=[jax.ShapeDtypeStruct((V, A), BF16)] * 2...  2.72 us

profile of v4, /device:TPU:16, one launch (start us, length us, event | category | flops | bytes accessed | tf_op | source)
XLA Modules:
  0.0 63.8 jit_solution(13196499399405451084)
XLA Ops:
  1.3 0.7 %broadcast_in_dim.7 = f32[8,512]{1,0:T(8,128)S(1)} broadcast(bf16[512]{0:T(512)(128)(2,1)} %param.7), dimensions={1} | broadcast | bytes 17408 | tf_op jit(solution)/shard_map/broadcast_in_dim | solution.py:401
  2.0 0.0 copy-start
  2.0 59.1 %window.1 = (bf16[512,2048]{1,0:T(8,128)(2,1)S(1)}, bf16[512,384]{1,0:T(8,128)(2,1)S(1)}) custom-call(bf16[512,2048]{1,0:T(8,128)(2,1)} %bitcast.7, f32[16,512]{1,0:T(8,128)S(1)} %concatenate.3.table, s32[3,1,32]{2,1,0:T(1,128)} %bitcast.11, s32[1,32]{1,0:T(1,128)} %count.1), custom_call_target="tpu_custom_call" | custom-call | flops 7516192768 | bytes 8388608 | tf_op jit(solution)/shard_map/window/pallas_call | solution.py:410
  61.1 0.0 copy-done
  61.1 2.7 %finish.1 = (bf16[512,2048]{1,0:T(8,128)(2,1)}, bf16[512,2048]{1,0:T(8,128)(2,1)}) custom-call(bf16[512,2048]{1,0:T(8,128)(2,1)S(1)} %bitcast.8, bf16[512,384]{1,0:T(8,128)(2,1)S(1)} %get-tuple-element.6.d, bf16[512,2048]{1,0:T(8,128)(2,1)S(1)} %get-tuple-element.7.g), custom_call_target="tpu_custom_call" | custom-call | flops 1073741824 | bytes 8388608 | tf_op jit(solution)/shard_map/finish/pallas_call | solution.py:446
  (1 shorter events, 0.0 us)
Async XLA Ops:
  2.0 59.1 %copy-start = (bf16[1,512,2048]{2,1,0:T(8,128)(2,1)S(1)}, bf16[1,512,2048]{2,1,0:T(8,128)(2,1)}, u32[]{:S(2)}) copy-start(bf16[1,512,2048]{2,1,0:T(8,128)(2,1)} %param.5) | copy-start | bytes 6291460

commit v5 on v4

--- a/solution.py
+++ b/solution.py
@@ -10,8 +10,8 @@
 MESH = pl.DeviceIdType.MESH
 NX, NY, NZ = 4, 4, 8
 CHUNKS = 16
-LEAD = 1
-FIRST = 4
+LEAD = 2
+FIRST = 5
 LAST = 384
 STEPS = 4
 FAR_FIRST = sorted(
@@ -329,14 +329,14 @@
         bulk_wait(2 * Q, 3 * Q)
         tile(2, 256, 128, far_energy)
         gamma(2, 0, LAST, w2)
-        bulk_wait(3 * Q, CHUNKS)
-        tile(2, LAST, 128, far_energy)
-        gamma_last(LAST, 128, w2)
         for dx in x_order:
             for dz in (0, 1, 7, 2, 6, 3, 5, 4):
                 if dx or dz:
                     full_arrival(dx * NZ + dz).wait_recv()
             fw_copy(dx).start()
+        bulk_wait(3 * Q, CHUNKS)
+        tile(2, LAST, 128, far_energy)
+        gamma_last(LAST, 128, w2)
 
     en1.wait_send()
     en2.wait_send()

time: 64.8 us -> 63.8 us (0.985)
  Pallas kernels: 61.8 us -> 61.1 us
    pallas_call x1, Pallas kernels: 59.1 us -> 58.4 us  [per_device(): pl.pallas_call(body, out_shape=[jax.ShapeDtypeStruct((V, A), BF16), jax.S...]
where the time goes in v5:
time: 63.8 us; the launch traced here: 63.1 us
  Pallas kernels  61.1 us (96%)
  between operations  1.3 us (2%)
  local copies, waits for them, and re-layouts  0.69 us (1%)
    pallas_call x1, Pallas kernels, per_device(): pl.pallas_call(body, out_shape=[jax.ShapeDtypeStruct((V, A), BF16), jax.S...  58.4 us
    pallas_call x1, Pallas kernels, per_device(): pl.pallas_call(finish, out_shape=[jax.ShapeDtypeStruct((V, A), BF16)] * 2...  2.72 us

profile of v5, /device:TPU:16, one launch (start us, length us, event | category | flops | bytes accessed | tf_op | source)
XLA Modules:
  0.0 63.1 jit_solution(3842340481996753390)
XLA Ops:
  1.3 0.7 %broadcast_in_dim.7 = f32[8,512]{1,0:T(8,128)S(1)} broadcast(bf16[512]{0:T(512)(128)(2,1)} %param.7), dimensions={1} | broadcast | bytes 17408 | tf_op jit(solution)/shard_map/broadcast_in_dim | solution.py:401
  2.0 0.0 copy-start
  2.0 58.4 %window.1 = (bf16[512,2048]{1,0:T(8,128)(2,1)S(1)}, bf16[512,384]{1,0:T(8,128)(2,1)S(1)}) custom-call(bf16[512,2048]{1,0:T(8,128)(2,1)} %bitcast.7, f32[16,512]{1,0:T(8,128)S(1)} %concatenate.3.table, s32[3,1,32]{2,1,0:T(1,128)} %bitcast.11, s32[1,32]{1,0:T(1,128)} %count.1), custom_call_target="tpu_custom_call" | custom-call | flops 7516192768 | bytes 8388608 | tf_op jit(solution)/shard_map/window/pallas_call | solution.py:410
  60.4 0.0 copy-done
  60.4 2.7 %finish.1 = (bf16[512,2048]{1,0:T(8,128)(2,1)}, bf16[512,2048]{1,0:T(8,128)(2,1)}) custom-call(bf16[512,2048]{1,0:T(8,128)(2,1)S(1)} %bitcast.8, bf16[512,384]{1,0:T(8,128)(2,1)S(1)} %get-tuple-element.6.d, bf16[512,2048]{1,0:T(8,128)(2,1)S(1)} %get-tuple-element.7.g), custom_call_target="tpu_custom_call" | custom-call | flops 1073741824 | bytes 8388608 | tf_op jit(solution)/shard_map/finish/pallas_call | solution.py:446
  (1 shorter events, 0.0 us)
Async XLA Ops:
  2.0 58.4 %copy-start = (bf16[1,512,2048]{2,1,0:T(8,128)(2,1)S(1)}, bf16[1,512,2048]{2,1,0:T(8,128)(2,1)}, u32[]{:S(2)}) copy-start(bf16[1,512,2048]{2,1,0:T(8,128)(2,1)} %param.5) | copy-start | bytes 6291460
